TPU v7x, 32 devices: a whole 2x2x4 slice. The times are simulated.
32 devices in a mesh: dp: 4 (over y, x), expert: 8 (over z, core).
Axes of the slice: x: 2, y: 2, z: 4, core: 2. Of those that a mesh axis runs over, the one named last changes fastest.
Arguments:
- tokens: bfloat16 [4096, 4096], P(('dp', 'expert')), may hold values from -6 to 6
- routes: int32 [4096, 2], P(('dp', 'expert')), may hold values from 0 to 7, all different within a row; in each aligned block of 128 rows (0 to 127, 128 to 255, ...) at most 48 rows name the same one
- router_weight: bfloat16 [4096, 8], replicated, may hold values from -0.09375 to 0.09375
- shift: float32 [1, 4096], replicated, may hold values from -3 to 3
- scale: float32 [1, 4096], replicated, may hold values from -3 to 3
- gate_mod: float32 [1, 4096], replicated, may hold values from -4 to 4
- gate_weight: bfloat16 [8, 4096, 1024], P(None, ('dp', 'expert')), may hold values from -0.09375 to 0.09375
- up_weight: bfloat16 [8, 4096, 1024], P(None, ('dp', 'expert')), may hold values from -0.09375 to 0.09375
- down_weight: bfloat16 [8, 4096, 1024], P(None, ('dp', 'expert')), may hold values from -0.1875 to 0.1875
Outputs:
- update: bfloat16 [4096, 4096], P(('dp', 'expert'))
Inputs may be any that keep to these rules, and one draw needn't show every extreme that they name: `routes`: each row names two different experts; among the rows of one device no expert is named more than 48 times, a bound that some block reaches.
All inputs are finite; a program needn't handle non-finite values.
Results may differ from a plain program's by a relative error of at most 0.0072.
Values may be sent and summed in bfloat16 or wider, within the bound.
A program may use at most 128 MiB of HBM per device.

v0:
```python
import jax
import jax.numpy as jnp
from jax import lax
from jax.sharding import PartitionSpec as P

PIX = 4096


EPS = 1e-06


def send_back(output):
    return lax.all_to_all(output, "expert", split_axis=0, concat_axis=0, tiled=True)


def shards(
    tokens, routes, router_weight, shift, scale, gate_mod, gate_weight, up_weight, down_weight
):
    tok_dev = tokens.shape[0]
    width = tokens.shape[1]
    experts = router_weight.shape[1]
    n_owner = lax.axis_size("expert")
    local_count = experts // n_owner
    capacity = max(2, 3 * tok_dev // experts)
    first_row = (lax.axis_index("dp") * n_owner + lax.axis_index("expert")) * tok_dev
    image = first_row // PIX
    shift_row = lax.dynamic_slice_in_dim(shift, image, 1, 0)
    scale_row = lax.dynamic_slice_in_dim(scale, image, 1, 0)
    gate_row = lax.dynamic_slice_in_dim(gate_mod, image, 1, 0)
    values = tokens.astype(jnp.float32)
    meansq = jnp.mean(values * values, axis=-1, keepdims=True)
    normed = (values * lax.rsqrt(meansq + EPS) * (1.0 + scale_row) + shift_row).astype(jnp.bfloat16)
    logits = jnp.dot(normed, router_weight, preferred_element_type=jnp.float32)
    onehot = routes[:, :, None] == jnp.arange(experts, dtype=jnp.int32)[None, None, :]
    chosen = jnp.sum(jnp.where(onehot, logits[:, None, :], 0.0), axis=-1)
    score = jax.nn.sigmoid(chosen)
    flat = routes.reshape(-1)
    hot = (flat[:, None] == jnp.arange(experts, dtype=jnp.int32)[None, :]).astype(jnp.int32)
    rank = jnp.cumsum(hot, axis=0) - hot
    slot = jnp.sum(rank * hot, axis=-1)
    position = flat * capacity + slot
    source = (
        jnp.zeros((experts * capacity,), jnp.int32)
        .at[position]
        .set(jnp.arange(2 * tok_dev, dtype=jnp.int32) // 2)
    )
    filled = jnp.zeros((experts * capacity,), jnp.bool_).at[position].set(True)
    outgoing = jnp.where(filled[:, None], normed[source], jnp.zeros((), jnp.bfloat16)).reshape(
        experts, capacity, width
    )
    quarter_gate, quarter_up, quarter_down = (
        lax.all_to_all(gate_weight, "expert", split_axis=0, concat_axis=1, tiled=True),
        lax.all_to_all(up_weight, "expert", split_axis=0, concat_axis=1, tiled=True),
        lax.all_to_all(down_weight, "expert", split_axis=0, concat_axis=1, tiled=True),
    )
    w_gate, w_up, w_down = (
        lax.all_gather(quarter_gate, "dp", axis=1, tiled=True),
        lax.all_gather(quarter_up, "dp", axis=1, tiled=True),
        lax.all_gather(quarter_down, "dp", axis=1, tiled=True),
    )
    received = lax.all_to_all(outgoing, "expert", split_axis=0, concat_axis=0, tiled=True)
    slots = received.shape[1]
    grid = received.reshape(n_owner, local_count, slots, width)
    gate = jnp.einsum("nxcd,xdf->nxcf", grid, w_gate, preferred_element_type=jnp.float32)
    upper = jnp.einsum("nxcd,xdf->nxcf", grid, w_up, preferred_element_type=jnp.float32)
    hidden = (jax.nn.silu(gate) * upper).astype(jnp.bfloat16)
    output = jnp.einsum(
        "nxcf,xdf->nxcd", hidden, w_down, preferred_element_type=jnp.float32
    ).astype(jnp.bfloat16)
    output = output.reshape(n_owner * local_count, slots, width)
    incoming = send_back(output)
    picked = (
        incoming.reshape(experts * capacity, width)[position]
        .astype(jnp.float32)
        .reshape(tok_dev, 2, width)
    )
    branch = jnp.sum(score[:, :, None] * picked, axis=1)
    return (gate_row * branch).astype(jnp.bfloat16)


def solution(mesh):
    in_specs = (
        P(("dp", "expert"), None),
        P(("dp", "expert"), None),
        P(),
        P(),
        P(),
        P(),
        P(None, ("dp", "expert"), None),
        P(None, ("dp", "expert"), None),
        P(None, ("dp", "expert"), None),
    )
    out_specs = P(("dp", "expert"), None)
    return jax.shard_map(shards, mesh=mesh, in_specs=in_specs, out_specs=out_specs, check_vma=False)
```

profile of v0, /device:TPU:0, one launch (start us, length us, event | category | flops | bytes accessed | tf_op | source)
XLA Modules:
  0.0 445.8 jit_solution(17261702014009396789)
XLA Ops:
  6.5 0.0 copy-start
  6.5 0.0 all-gather.4.cloned.1.call-start
  6.5 55.6 %all_to_all.46 = bf16[8,128,1024]{2,1,0:T(8,128)(2,1)} all-to-all(bf16[8,128,1024]{2,1,0:T(8,128)(2,1)} %param.15), channel_id=1, replica_groups=mesh['dp'=4,'expert'=8] {'expert'}, dimensions={0} | all-to-all | bytes 4194304 | tf_op jit(solution)/shard_map/all_to_all | solution.py:52
  62.2 0.0 all-gather.4.cloned.1.call-update
  62.2 0.0 all-gather.6.cloned.1.call-start
  62.2 0.0 copy-done.2
  62.2 52.2 %all_to_all.47 = bf16[8,128,1024]{2,1,0:T(8,128)(2,1)} all-to-all(bf16[8,128,1024]{2,1,0:T(8,128)(2,1)S(1)} %copy-done.2), channel_id=1, replica_groups=mesh['dp'=4,'expert'=8] {'expert'}, dimensions={0} | all-to-all | bytes 4194304 | tf_op jit(solution)/shard_map/all_to_all | solution.py:53
  114.4 0.0 all-gather.6.cloned.1.call-update
  114.5 0.0 copy-start.7
  114.5 0.0 copy-start.1
  114.5 0.0 copy-start.6
  114.5 0.0 copy-start.4
  114.5 0.0 all-gather.8.cloned.1.call-start
  114.6 1.5 copy-done.3
  116.0 52.2 %all_to_all.48 = bf16[8,128,1024]{2,1,0:T(8,128)(2,1)} all-to-all(bf16[8,128,1024]{2,1,0:T(8,128)(2,1)S(1)} %copy-done.3), channel_id=1, replica_groups=mesh['dp'=4,'expert'=8] {'expert'}, dimensions={0} | all-to-all | bytes 4194304 | tf_op jit(solution)/shard_map/all_to_all | solution.py:54
  168.2 0.0 all-gather.8.cloned.1.call-update
  168.2 0.0 copy-done.7
  168.2 0.1 copy.19
  168.4 0.1 eq.45
  168.5 0.1 eq.41
  168.7 0.6 reduce-window.6
  169.2 0.2 slice_reduce_fusion
  169.5 0.1 copy.18
  169.6 0.1 mul.78
  169.8 0.1 fusion.26
  169.9 1.4 scatter_custom_fusion.1
  171.3 1.5 scatter_custom_fusion
  172.8 0.1 broadcast_in_dim.49
  172.9 0.0 copy-done.1
  172.9 0.3 fusion.9
  173.2 0.0 copy-done.6
  173.2 0.0 copy-done.4
  173.2 0.4 fusion.12
  173.6 4.0 gather_fusion
  177.7 2.2 broadcast_select_fusion
  179.8 74.8 %all_to_all.49 = bf16[8,48,4096]{2,1,0:T(8,128)(2,1)} all-to-all(bf16[8,48,4096]{2,1,0:T(8,128)(2,1)S(1)} %broadcast_select_fusion), channel_id=1, replica_groups=mesh['dp'=4,'expert'=8] {'expert'}, dimensions={0} | all-to-all | bytes 6291456 | tf_op jit(solution)/shard_map/all_to_all | solution.py:61
  254.6 8.9 %fusion.4 = f32[8,48,1024]{2,1,0:T(8,128)} fusion(bf16[8,48,4096]{2,1,0:T(8,128)(2,1)} %all_to_all.49, bf16[1,4096,1024]{2,1,0:T(8,128)(2,1)} %all-gather.4.cloned.1.call-done), kind=kOutput, calls=%fused_computation.8 | convolution fusion | flops 3221225472 | bytes 13107200 | tf_op jit(solution)/shard_map/nxcd,xdf->nxcf/dot_general | solution.py:64
  263.5 64.0 %all-gather.8.cloned.1.call-done = bf16[1,4096,1024]{2,1,0:T(8,128)(2,1)} async-done(((bf16[1,1024,1024]{2,1,0:T(8,128)(2,1)}), bf16[1,4096,1024]{2,1,0:T(8,128)(2,1)}) %all-gather.8.cloned.1.call-update) | async-done | bytes 8388624 | tf_op jit(solution)/shard_map/all_gather | solution.py:59
  327.5 15.5 %fusion.6 = bf16[8,48,4096]{2,1,0:T(8,128)(2,1)} fusion(bf16[1,4096,1024]{2,1,0:T(8,128)(2,1)} %all-gather.8.cloned.1.call-done, bf16[8,48,4096]{2,1,0:T(8,128)(2,1)} %all_to_all.49, bf16[1,4096,1024]{2,1,0:T(8,128)(2,1)} %all-gather.6.cloned.1.call-done, f32[8,48,1024]{2,1,0:T(8,128)} %fusion.4), kind=kOutput, calls=%fused_computation.10 | convolution fusion | flops 6446383104 | bytes 24641536 | tf_op jit(solution)/shard_map/nxcf,xdf->nxcd/dot_general | solution.py:67
  343.0 4.7 %all-to-all-start.4 = ((bf16[8,48,4096]{2,1,0:T(8,128)(2,1)}), bf16[8,48,4096]{2,1,0:T(8,128)(2,1)}, u32[]{:S(2)}, u32[]{:S(2)}) async-start(bf16[8,48,4096]{2,1,0:T(8,128)(2,1)} %fusion.6), calls=%async_computation.4 | async-start | bytes 6291456 | tf_op jit(solution)/shard_map/all_to_all | solution.py:13
  347.7 0.0 copy-done
  347.7 0.4 fusion.33
  348.1 0.1 copy.17
  348.2 71.0 %all-to-all-done.4 = bf16[8,48,4096]{2,1,0:T(8,128)(2,1)} async-done(((bf16[8,48,4096]{2,1,0:T(8,128)(2,1)}), bf16[8,48,4096]{2,1,0:T(8,128)(2,1)}, u32[]{:S(2)}, u32[]{:S(2)}) %all-to-all-start.4) | async-done | bytes 3145760 | tf_op jit(solution)/shard_map/all_to_all | solution.py:13
  419.2 6.2 %gather_fusion.1 = bf16[256,4096]{1,0:T(8,128)(2,1)S(1)} fusion(bf16[384,4096]{1,0:T(8,128)(2,1)} %bitcast.26, s32[1024]{0:T(1024)S(1)} %pad_clamp_fusion), kind=kCustom, calls=%fused_computation.1 | custom fusion | bytes 4195328 | tf_op jit(solution)/shard_map/gather | solution.py:73
  425.4 4.0 reshape.114
  429.4 8.7 %multiply_reduce_fusion = f32[128,4096]{1,0:T(8,128)S(1)} fusion(f32[128,2,4096]{2,1,0:T(2,128)} %reshape.114, f32[128,2]{1,0:T(8,128)S(1)} %copy.17), kind=kLoop, calls=%fused_computation.11 | loop fusion | flops 1572864 | bytes 6292480 | tf_op jit(solution)/shard_map/reduce_sum | solution.py:77
  438.2 1.1 multiply_convert_fusion
  (20 shorter events, 0.1 us)
Async XLA Ops:
  6.5 341.1 %copy-start = (bf16[4096,8]{0,1:T(8,128)(2,1)S(1)}, bf16[4096,8]{0,1:T(8,128)(2,1)}, u32[]{:S(2)}) copy-start(bf16[4096,8]{0,1:T(8,128)(2,1)} %param.11) | copy-start | bytes 196612
  6.5 55.7 %copy-start.2 = (bf16[8,128,1024]{2,1,0:T(8,128)(2,1)S(1)}, bf16[8,128,1024]{2,1,0:T(8,128)(2,1)}, u32[]{:S(2)}) copy-start(bf16[8,128,1024]{2,1,0:T(8,128)(2,1)} %param.16) | copy-start | bytes 6291460
  6.5 248.0 %all-gather.4.cloned.1.call-start = ((), (), s32[]{:S(2)}) async-start(), calls=%async_computation.5 | async-start | bytes 10485760 | tf_op jit(solution)/shard_map/all_gather | solution.py:57
  62.2 201.3 %all-gather.6.cloned.1.call-start = ((), (), s32[]{:S(2)}) async-start(), calls=%async_computation.6 | async-start | bytes 10485760 | tf_op jit(solution)/shard_map/all_gather | solution.py:58
  114.4 1.6 copy-start.3
  114.5 53.8 %copy-start.7 = (s32[128,2]{0,1:T(2,128)S(1)}, s32[128,2]{0,1:T(2,128)}, u32[]{:S(2)}) copy-start(s32[128,2]{0,1:T(2,128)} %param.10) | copy-start | bytes 3076
  114.5 58.4 %copy-start.1 = (bf16[128,4096]{1,0:T(8,128)(2,1)S(1)}, bf16[128,4096]{1,0:T(8,128)(2,1)}, u32[]{:S(2)}) copy-start(bf16[128,4096]{1,0:T(8,128)(2,1)} %param.9) | copy-start | bytes 3145732
  114.5 58.7 %copy-start.6 = (f32[1,4096]{1,0:T(1,128)S(1)}, f32[1,4096]{1,0:T(1,128)}, u32[]{:S(2)}) copy-start(f32[1,4096]{1,0:T(1,128)} %param.13) | copy-start | bytes 49156
  114.5 58.7 %copy-start.4 = (f32[1,4096]{1,0:T(1,128)S(1)}, f32[1,4096]{1,0:T(1,128)}, u32[]{:S(2)}) copy-start(f32[1,4096]{1,0:T(1,128)} %param.12) | copy-start | bytes 49156
  114.5 213.0 %all-gather.8.cloned.1.call-start = ((), (), s32[]{:S(2)}) async-start(), calls=%async_computation.7 | async-start | bytes 10485760 | tf_op jit(solution)/shard_map/all_gather | solution.py:59
  343.0 76.2 %all-to-all-start.4 = ((bf16[8,48,4096]{2,1,0:T(8,128)(2,1)}), bf16[8,48,4096]{2,1,0:T(8,128)(2,1)}, u32[]{:S(2)}, u32[]{:S(2)}) async-start(bf16[8,48,4096]{2,1,0:T(8,128)(2,1)} %fusion.6), calls=%async_computation.4 | async-start | bytes 6291456 | tf_op jit(solution)/shard_map/all_to_all | solution.py:13
  429.4 8.8 %copy-start.5 = (f32[1,4096]{1,0:T(1,128)S(1)}, f32[1,4096]{1,0:T(1,128)}, u32[]{:S(2)}) copy-start(f32[1,4096]{1,0:T(1,128)} %param.14) | copy-start | bytes 49156
Sparse Core Ops, SparseCore 0:
  62.3 86.4 all-gather.3
  150.6 87.4 all-gather.5
  240.0 87.4 all-gather.7
where the time goes:
time: 446 us
  blocking collectives  235 us (53%)
  waiting for transfers between devices  135 us (30%)
  matrix products  24.8 us (6%)
  local copies, waits for them, and re-layouts  19.7 us (4%)
  other arithmetic  13.5 us (3%)
  between operations  13.3 us (3%)
  starting transfers between devices  4.74 us (1%)
    all_to_all x1, blocking collectives, shards(): lax.all_to_all(outgoing, 'expert', split_axis=0, concat_axis=0, tiled=True)  74.8 us
    all_to_all x1, waiting for transfers between devices, send_back(): lax.all_to_all(output, 'expert', split_axis=0, concat_axis=0, tiled=True)  71 us
    all_gather x1, waiting for transfers between devices, shards(): lax.all_gather(quarter_down, 'dp', axis=1, tiled=True)  64 us
    all_to_all x1, blocking collectives, shards(): lax.all_to_all(gate_weight, 'expert', split_axis=0, concat_axis=1, tiled=...  55.6 us
    all_to_all x1, blocking collectives, shards(): lax.all_to_all(up_weight, 'expert', split_axis=0, concat_axis=1, tiled=True)  52.2 us
    all_to_all x1, blocking collectives, shards(): lax.all_to_all(down_weight, 'expert', split_axis=0, concat_axis=1, tiled=...  52.2 us
    dot_general x1, matrix products, shards(): jnp.einsum('nxcf,xdf->nxcd', hidden, w_down, preferred_element_type=jnp.f...  15.5 us
  transfers between devices with their start and end apart: 4, of which 2 were waited for; matrix products, arithmetic and copies ran while one was open for 5% of the time, Pallas kernels for 0%

commit v1 on v0

--- a/solution.py
+++ b/solution.py
@@ -1,6 +1,10 @@
+import functools
+
 import jax
 import jax.numpy as jnp
 from jax import lax
+from jax.experimental import pallas as pl
+from jax.experimental.pallas import tpu as pltpu
 from jax.sharding import PartitionSpec as P
 
 PIX = 4096
@@ -13,7 +17,7 @@
     return lax.all_to_all(output, "expert", split_axis=0, concat_axis=0, tiled=True)
 
 
-def shards(
+def shards_plain(
     tokens, routes, router_weight, shift, scale, gate_mod, gate_weight, up_weight, down_weight
 ):
     tok_dev = tokens.shape[0]
@@ -78,6 +82,262 @@
     return (gate_row * branch).astype(jnp.bfloat16)
 
 
+MESH = pl.DeviceIdType.MESH
+
+
+def wait_bytes(ref, sem):
+    pltpu.make_async_copy(ref, ref, sem).wait()
+
+
+def kernel(
+    n_dp, n_owner, tok_ref, router_ref, routes_ref, shift_ref, scale_ref, gmod_ref, disp_ref, comb_ref,
+    gate_ref, up_ref, down_ref, out_ref,
+    weights, normed, outgoing, rows, gate_acc, hidden, obuf, incoming, score_ref,
+    z_send, w_recv, xy_send, t_send, t_recv, o_send, o_recv,
+):
+    dp, me = lax.axis_index("dp"), lax.axis_index("expert")
+    x_dp = dp + 1 - 2 * (dp % 2)
+    y_dp = (dp + 2) % n_dp
+    d_dp = n_dp - 1 - dp
+    tok_dev, width = tok_ref.shape
+    capacity = disp_ref.shape[1]
+    depth, units = gate_ref.shape[1], gate_ref.shape[2]
+    args = (gate_ref, up_ref, down_ref)
+
+    barrier = pltpu.get_barrier_semaphore()
+    for r in range(1, n_owner):
+        pl.semaphore_signal(barrier, inc=1, device_id=(dp, (me + r) % n_owner), device_id_type=MESH)
+    pl.semaphore_signal(barrier, inc=1, device_id=(x_dp, me), device_id_type=MESH)
+    pl.semaphore_signal(barrier, inc=1, device_id=(y_dp, me), device_id_type=MESH)
+    pl.semaphore_wait(barrier, n_owner + 1)
+
+    def own(a):
+        return pltpu.make_async_copy(args[a].at[me], weights.at[a, dp * n_owner + me], w_recv.at[a, 0, 0])
+
+    def send_column(a):
+        own(a).start()
+        for r in range(1, n_owner):
+            to = (me + r) % n_owner
+            pltpu.make_async_remote_copy(
+                src_ref=args[a].at[to], dst_ref=weights.at[a, dp * n_owner + me],
+                send_sem=z_send.at[a], recv_sem=w_recv.at[a, r, 0],
+                device_id=(dp, to), device_id_type=MESH,
+            ).start()
+
+    def piece(a, r, part):
+        return weights.at[a, part * n_owner + (me + n_owner - r) % n_owner]
+
+    def spread(a, r, part, to, slot, kind):
+        pltpu.make_async_remote_copy(
+            src_ref=piece(a, r, part), dst_ref=piece(a, r, part),
+            send_sem=xy_send.at[a, kind], recv_sem=w_recv.at[a, r, slot],
+            device_id=(to, me), device_id_type=MESH,
+        ).start()
+
+    def arrived(a, r, part, slot):
+        wait_bytes(piece(a, r, part), w_recv.at[a, r, slot])
+
+    def relay(a, r):
+        arrived(a, r, dp, 0)
+        spread(a, r, dp, x_dp, 1, 0)
+        spread(a, r, dp, y_dp, 2, 1)
+
+    def corner(a, r):
+        arrived(a, r, x_dp, 1)
+        if r % 2 == 0:
+            spread(a, r, x_dp, y_dp, 3, 2)
+        arrived(a, r, y_dp, 2)
+        if r % 2 == 1:
+            spread(a, r, y_dp, x_dp, 3, 2)
+
+    send_column(0)
+    relay(0, 0)
+
+    block = 16
+
+    @pl.loop(0, tok_dev // block)
+    def _(i):
+        at = pl.ds(pl.multiple_of(i * block, block), block)
+        values = tok_ref[at, :].astype(jnp.float32)
+        meansq = jnp.mean(values * values, axis=-1, keepdims=True)
+        fresh = values * lax.rsqrt(meansq + EPS) * (1.0 + scale_ref[...]) + shift_ref[...]
+        normed[at, :] = fresh.astype(jnp.bfloat16)
+
+    for r in range(n_owner):
+        to = (me + r) % n_owner
+        picked = jnp.dot(disp_ref[to], normed[...], preferred_element_type=jnp.float32).astype(jnp.bfloat16)
+        if r == 0:
+            rows[me] = picked
+        else:
+            outgoing[r - 1] = picked
+            pltpu.make_async_remote_copy(
+                src_ref=outgoing.at[r - 1], dst_ref=rows.at[me],
+                send_sem=t_send.at[0], recv_sem=t_recv.at[r],
+                device_id=(dp, to), device_id_type=MESH,
+            ).start()
+    send_column(1)
+    send_column(2)
+
+    logits = jnp.dot(normed[...], router_ref[...], preferred_element_type=jnp.float32)
+    names = lax.broadcasted_iota(jnp.int32, logits.shape, 1)
+    for k in range(2):
+        chosen = jnp.sum(jnp.where(routes_ref[:, k : k + 1] == names, logits, 0.0), axis=-1, keepdims=True)
+        score_ref[k] = jnp.broadcast_to(jax.nn.sigmoid(chosen), score_ref.shape[1:])
+
+    tile = 256
+
+    def product(a, at):
+        part = weights[a, :, :, at].reshape(width, tile)
+        grid = rows[...].reshape(n_owner * capacity, width)
+        return jnp.dot(grid, part, preferred_element_type=jnp.float32)
+
+    lag = 2
+    for a in range(2):
+        for r in range(n_owner + lag):
+            if 0 < r < n_owner:
+                relay(a, r)
+            if r >= lag:
+                corner(a, r - lag)
+        for r in range(n_owner):
+            arrived(a, r, d_dp, 3)
+        relay(a + 1, 0)
+        if a == 0:
+            for r in range(1, n_owner):
+                wait_bytes(rows.at[(me + n_owner - r) % n_owner], t_recv.at[r])
+
+        @pl.loop(0, units // tile)
+        def _(i):
+            at = pl.ds(pl.multiple_of(i * tile, tile), tile)
+            if a == 0:
+                gate_acc[:, at] = product(0, at)
+            else:
+                gate = gate_acc[:, at]
+                hidden[:, at] = (jax.nn.silu(gate) * product(1, at)).astype(jnp.bfloat16)
+
+    def finish(r):
+        arrived(2, r, d_dp, 3)
+        source = (me + n_owner - r) % n_owner
+        for q in range(n_dp):
+            part = weights[2, q * n_owner + source]
+            result = lax.dot_general(
+                hidden[...], part, (((1,), (1,)), ((), ())), preferred_element_type=jnp.float32
+            ).astype(jnp.bfloat16)
+            obuf[r, :, :, q * depth : (q + 1) * depth] = result.reshape(n_owner, capacity, depth)
+        incoming[source, me] = obuf[r, me]
+        for t in range(1, n_owner):
+            to = (me + t) % n_owner
+            pltpu.make_async_remote_copy(
+                src_ref=obuf.at[r, to], dst_ref=incoming.at[source, me],
+                send_sem=o_send.at[r], recv_sem=o_recv.at[r, t],
+                device_id=(dp, to), device_id_type=MESH,
+            ).start()
+
+    far = 2
+    for r in range(n_owner + lag + far):
+        if 0 < r < n_owner:
+            relay(2, r)
+        if lag <= r < n_owner + lag:
+            corner(2, r - lag)
+        if r >= lag + far:
+            finish(r - lag - far)
+
+    for r in range(n_owner):
+        for t in range(1, n_owner):
+            sender = (me + n_owner - t) % n_owner
+            source = (me + 2 * n_owner - t - r) % n_owner
+            wait_bytes(incoming.at[source, sender], o_recv.at[r, t])
+
+    for source in range(n_owner):
+        block_in = incoming[source].reshape(n_owner * capacity, n_dp * depth)
+        first = jnp.dot(comb_ref[0], block_in, preferred_element_type=jnp.float32)
+        second = jnp.dot(comb_ref[1], block_in, preferred_element_type=jnp.float32)
+        for q in range(n_dp):
+            cols = slice(q * depth, (q + 1) * depth)
+            at = slice((q * n_owner + source) * depth, (q * n_owner + source + 1) * depth)
+            branch = score_ref[0] * first[:, cols] + score_ref[1] * second[:, cols]
+            out_ref[:, at] = (gmod_ref[:, at] * branch).astype(jnp.bfloat16)
+
+    for a in range(3):
+        wait_bytes(args[a].at[pl.ds(0, n_owner - 1)], z_send.at[a])
+        for kind in range(3):
+            wait_bytes(weights.at[a, pl.ds(0, n_owner)], xy_send.at[a, kind])
+    wait_bytes(outgoing, t_send.at[0])
+    for r in range(n_owner):
+        wait_bytes(obuf.at[r, pl.ds(0, n_owner - 1)], o_send.at[r])
+
+
+def shards(
+    n_dp, n_owner, tokens, routes, router_weight, shift, scale, gate_mod, gate_weight, up_weight, down_weight
+):
+    tok_dev, width = tokens.shape
+    experts, depth, units = gate_weight.shape
+    capacity = max(2, 3 * tok_dev // experts)
+    first_row = (lax.axis_index("dp") * n_owner + lax.axis_index("expert")) * tok_dev
+    image = first_row // PIX if shift.shape[0] > 1 else 0
+    shift_row = lax.dynamic_slice_in_dim(shift, image, 1, 0)
+    scale_row = lax.dynamic_slice_in_dim(scale, image, 1, 0)
+    gate_row = lax.dynamic_slice_in_dim(gate_mod, image, 1, 0)
+    hot = routes[:, :, None] == jnp.arange(experts, dtype=jnp.int32)[None, None, :]
+    named = jnp.sum(hot.astype(jnp.bfloat16), axis=1)
+    order = jnp.arange(tok_dev)
+    below = (order[:, None] > order[None, :]).astype(jnp.bfloat16)
+    rank = jnp.dot(below, named, preferred_element_type=jnp.float32)
+    slot = jnp.sum(jnp.where(hot, rank[:, None, :], 0.0), axis=-1).astype(jnp.int32)
+    position = routes * capacity + slot
+    places = jnp.arange(experts * capacity, dtype=jnp.int32)
+    comb = (position.T[:, :, None] == places[None, None, :]).astype(jnp.bfloat16)
+    turned = position.T[:, None, :] == places[None, :, None]
+    disp = (turned[0] | turned[1]).astype(jnp.bfloat16).reshape(experts, capacity, tok_dev)
+    vmem = pl.BlockSpec(memory_space=pltpu.VMEM)
+    hbm = pl.BlockSpec(memory_space=pl.ANY)
+    grid_rows = n_owner * capacity
+    return pl.pallas_call(
+        functools.partial(kernel, n_dp, n_owner),
+        out_shape=jax.ShapeDtypeStruct((tok_dev, width), jnp.bfloat16),
+        in_specs=[vmem] * 8 + [hbm] * 3,
+        out_specs=vmem,
+        scratch_shapes=[
+            pltpu.VMEM((3, n_dp * n_owner, depth, units), jnp.bfloat16),
+            pltpu.VMEM((tok_dev, width), jnp.bfloat16),
+            pltpu.VMEM((n_owner - 1, capacity, width), jnp.bfloat16),
+            pltpu.VMEM((n_owner, capacity, width), jnp.bfloat16),
+            pltpu.VMEM((grid_rows, units), jnp.float32),
+            pltpu.VMEM((grid_rows, units), jnp.bfloat16),
+            pltpu.VMEM((n_owner, n_owner, capacity, n_dp * depth), jnp.bfloat16),
+            pltpu.VMEM((n_owner, n_owner, capacity, n_dp * depth), jnp.bfloat16),
+            pltpu.VMEM((2, tok_dev, depth), jnp.float32),
+            pltpu.SemaphoreType.DMA((3,)),
+            pltpu.SemaphoreType.DMA((3, n_owner, 4)),
+            pltpu.SemaphoreType.DMA((3, 3)),
+            pltpu.SemaphoreType.DMA((1,)),
+            pltpu.SemaphoreType.DMA((n_owner,)),
+            pltpu.SemaphoreType.DMA((n_owner,)),
+            pltpu.SemaphoreType.DMA((n_owner, n_owner)),
+        ],
+        compiler_params=pltpu.CompilerParams(
+            collective_id=0, has_side_effects=True, vmem_limit_bytes=64000 * 1024
+        ),
+    )(
+        tokens, router_weight, routes, shift_row, scale_row, gate_row, disp, comb,
+        gate_weight, up_weight, down_weight,
+    )
+
+
+def choose(mesh):
+    n_dp, n_owner = mesh.shape["dp"], mesh.shape["expert"]
+
+    def body(*args):
+        tokens, weight = args[0], args[6]
+        capacity = max(2, 3 * tokens.shape[0] // weight.shape[0])
+        fits = n_dp == 4 and weight.shape[0] == n_owner and n_owner % 2 == 0
+        fits = fits and capacity % 16 == 0 and weight.shape[1] % 128 == 0 and tokens.shape[0] % 16 == 0
+        if fits:
+            return shards(n_dp, n_owner, *args)
+        return shards_plain(*args)
+
+    return body
+
+
 def solution(mesh):
     in_specs = (
         P(("dp", "expert"), None),
@@ -91,4 +351,5 @@
         P(None, ("dp", "expert"), None),
     )
     out_specs = P(("dp", "expert"), None)
-    return jax.shard_map(shards, mesh=mesh, in_specs=in_specs, out_specs=out_specs, check_vma=False)
+    return jax.shard_map(
+        choose(mesh), mesh=mesh, in_specs=in_specs, out_specs=out_specs, check_vma=False)

time: 446 us -> 338 us (0.76)
  Pallas kernels: 0 us -> 328 us
  blocking collectives: 235 us -> 0 us
  waiting for transfers between devices: 135 us -> 0 us
  matrix products: 24.8 us -> 0.13 us
  local copies, waits for them, and re-layouts: 19.7 us -> 5.84 us
  between operations: 13.3 us -> 0.02 us
  other arithmetic: 13.5 us -> 3.6 us
  starting transfers between devices: 4.74 us -> 0 us
    pallas_call x0 -> x1, Pallas kernels: none -> 328 us  [shards(): pl.pallas_call(functools.partial(kernel, n_dp, n_owner), out_shape=jax.Sh...]
    all_to_all x4 -> x0, blocking collectives: 235 us -> none  [the longest x1 74.8 us: shards(): lax.all_to_all(outgoing, 'expert', split_axis=0, concat_axis=0, tiled=True)]
    all_to_all x1 -> x0, waiting for transfers between devices: 71 us -> none  [send_back(): lax.all_to_all(output, 'expert', split_axis=0, concat_axis=0, tiled=True)]
    all_gather x3 -> x0, waiting for transfers between devices: 64 us -> none  [the longest x1 64 us: shards(): lax.all_gather(quarter_down, 'dp', axis=1, tiled=True)]
    dot_general x3 -> x1, matrix products: 24.8 us -> 0.13 us  [shards(): rank = jnp.dot(below, named, preferred_element_type=jnp.float32)]
    gather x2 -> x0, local copies, waits for them, and re-layouts: 10.2 us -> none  [the longest x1 6.18 us: shards(): incoming.reshape(experts * capacity, width)[position].astype(jnp.float32)]
    reduce_sum x4 -> x2, other arithmetic: 9.14 us -> 1.4 us  [the longest x1 0.72 us: shards(): jnp.sum(jnp.where(hot, rank[:, None, :], 0.0), axis=-1).astype(jnp.int32)]
    all_to_all x1 -> x0, starting transfers between devices: 4.66 us -> none  [send_back(): lax.all_to_all(output, 'expert', split_axis=0, concat_axis=0, tiled=True)]
  transfers between devices with their start and end apart: 4 -> 0, of which waited for: 2 -> 0; matrix products, arithmetic and copies ran while one was open for 5% -> 0% of each run, Pallas kernels for 0% -> 0%
where the time goes in v1:
time: 338 us; the launch traced here: 337 us
  Pallas kernels  328 us (97%)
  local copies, waits for them, and re-layouts  5.84 us (2%)
  other arithmetic  3.6 us (1%)
    pallas_call x1, Pallas kernels, shards(): pl.pallas_call(functools.partial(kernel, n_dp, n_owner), out_shape=jax.Sh...  328 us

profile of v1, /device:TPU:0, one launch (start us, length us, event | category | flops | bytes accessed | tf_op | source)
XLA Modules:
  0.0 337.4 jit_solution(10551647591469025356)
XLA Ops:
  0.0 0.7 fusion.4
  0.7 0.1 fusion.2
  0.8 0.7 select_reduce_fusion
  1.5 0.7 add_bitcast_fusion
  2.2 1.4 copy.15.routes_ref
  3.6 0.1 iota_compare_fusion.1
  3.7 0.7 fusion.1
  4.4 0.8 fusion.comb_ref
  5.1 2.2 copy.14.router_ref
  7.3 327.8 %shard_map.91 = bf16[128,4096]{1,0:T(8,128)(2,1)} custom-call(bf16[128,4096]{1,0:T(8,128)(2,1)} %tok_ref.1, bf16[4096,8]{1,0:T(8,128)(2,1)} %copy.14.router_ref, s32[128,2]{1,0:T(8,128)} %copy.15.routes_ref, f32[1,4096]{1,0:T(1,128)} %shift_ref.1, f32[1,4096]{1,0:T(1,128)} %scale_ref.1, f32[1,4096]{1,0:T(1,128)} %gmod_ref.1, bf16[8,48,128]{2,1,0:T(8,128)(2,1)} %bitcast.4, ...), custom_call_target="tpu_custom_call" | custom-call | tf_op jit(solution)/shard_map/pallas_call | solution.py:294
  335.1 2.3 copy.17

commit v2 on v1

v2 whole, which is shorter than its diff:
```python
import functools

import jax
import jax.numpy as jnp
from jax import lax
from jax.experimental import pallas as pl
from jax.experimental.pallas import tpu as pltpu
from jax.sharding import PartitionSpec as P

PIX = 4096


EPS = 1e-06

LAG, FAR = 2, 1
FAR_TOKENS, GATE_AT = 2, 3


def send_back(output):
    return lax.all_to_all(output, "expert", split_axis=0, concat_axis=0, tiled=True)


def shards_plain(
    tokens, routes, router_weight, shift, scale, gate_mod, gate_weight, up_weight, down_weight
):
    tok_dev = tokens.shape[0]
    width = tokens.shape[1]
    experts = router_weight.shape[1]
    n_owner = lax.axis_size("expert")
    local_count = experts // n_owner
    capacity = max(2, 3 * tok_dev // experts)
    first_row = (lax.axis_index("dp") * n_owner + lax.axis_index("expert")) * tok_dev
    image = first_row // PIX
    shift_row = lax.dynamic_slice_in_dim(shift, image, 1, 0)
    scale_row = lax.dynamic_slice_in_dim(scale, image, 1, 0)
    gate_row = lax.dynamic_slice_in_dim(gate_mod, image, 1, 0)
    values = tokens.astype(jnp.float32)
    meansq = jnp.mean(values * values, axis=-1, keepdims=True)
    normed = (values * lax.rsqrt(meansq + EPS) * (1.0 + scale_row) + shift_row).astype(jnp.bfloat16)
    logits = jnp.dot(normed, router_weight, preferred_element_type=jnp.float32)
    onehot = routes[:, :, None] == jnp.arange(experts, dtype=jnp.int32)[None, None, :]
    chosen = jnp.sum(jnp.where(onehot, logits[:, None, :], 0.0), axis=-1)
    score = jax.nn.sigmoid(chosen)
    flat = routes.reshape(-1)
    hot = (flat[:, None] == jnp.arange(experts, dtype=jnp.int32)[None, :]).astype(jnp.int32)
    rank = jnp.cumsum(hot, axis=0) - hot
    slot = jnp.sum(rank * hot, axis=-1)
    position = flat * capacity + slot
    source = (
        jnp.zeros((experts * capacity,), jnp.int32)
        .at[position]
        .set(jnp.arange(2 * tok_dev, dtype=jnp.int32) // 2)
    )
    filled = jnp.zeros((experts * capacity,), jnp.bool_).at[position].set(True)
    outgoing = jnp.where(filled[:, None], normed[source], jnp.zeros((), jnp.bfloat16)).reshape(
        experts, capacity, width
    )
    quarter_gate, quarter_up, quarter_down = (
        lax.all_to_all(gate_weight, "expert", split_axis=0, concat_axis=1, tiled=True),
        lax.all_to_all(up_weight, "expert", split_axis=0, concat_axis=1, tiled=True),
        lax.all_to_all(down_weight, "expert", split_axis=0, concat_axis=1, tiled=True),
    )
    w_gate, w_up, w_down = (
        lax.all_gather(quarter_gate, "dp", axis=1, tiled=True),
        lax.all_gather(quarter_up, "dp", axis=1, tiled=True),
        lax.all_gather(quarter_down, "dp", axis=1, tiled=True),
    )
    received = lax.all_to_all(outgoing, "expert", split_axis=0, concat_axis=0, tiled=True)
    slots = received.shape[1]
    grid = received.reshape(n_owner, local_count, slots, width)
    gate = jnp.einsum("nxcd,xdf->nxcf", grid, w_gate, preferred_element_type=jnp.float32)
    upper = jnp.einsum("nxcd,xdf->nxcf", grid, w_up, preferred_element_type=jnp.float32)
    hidden = (jax.nn.silu(gate) * upper).astype(jnp.bfloat16)
    output = jnp.einsum(
        "nxcf,xdf->nxcd", hidden, w_down, preferred_element_type=jnp.float32
    ).astype(jnp.bfloat16)
    output = output.reshape(n_owner * local_count, slots, width)
    incoming = send_back(output)
    picked = (
        incoming.reshape(experts * capacity, width)[position]
        .astype(jnp.float32)
        .reshape(tok_dev, 2, width)
    )
    branch = jnp.sum(score[:, :, None] * picked, axis=1)
    return (gate_row * branch).astype(jnp.bfloat16)


MESH = pl.DeviceIdType.MESH


def wait_bytes(ref, sem):
    pltpu.make_async_copy(ref, ref, sem).wait()


def kernel(
    n_dp, n_owner, tok_ref, router_ref, routes_ref, place_ref, shift_ref, scale_ref, gmod_ref,
    gate_ref, up_ref, down_ref, out_ref,
    weights, normed, far_tok, meta, outgoing, rows, gate_acc, hidden, obuf, incoming, comb, dense, land,
    z_send, w_recv, xy_send, f_send, f_recv, t_send, t_recv, h_sem, o_send, o_recv, d_send, d_recv,
):
    dp, me = lax.axis_index("dp"), lax.axis_index("expert")
    x_dp = dp + 1 - 2 * (dp % 2)
    y_dp = (dp + 2) % n_dp
    d_dp = n_dp - 1 - dp
    n_half = n_owner // 2
    half, low = me // n_half, me % n_half
    other = 1 - half
    mirror = other * n_half + low
    tok_dev, width = tok_ref.shape
    capacity = outgoing.shape[2]
    depth, units = gate_ref.shape[1], gate_ref.shape[2]
    args = (gate_ref, up_ref, down_ref)

    barrier = pltpu.get_barrier_semaphore()
    for r in range(1, n_owner):
        pl.semaphore_signal(barrier, inc=1, device_id=(dp, (me + r) % n_owner), device_id_type=MESH)
    pl.semaphore_signal(barrier, inc=1, device_id=(x_dp, me), device_id_type=MESH)
    pl.semaphore_signal(barrier, inc=1, device_id=(y_dp, me), device_id_type=MESH)
    pl.semaphore_wait(barrier, n_owner + 1)

    def remote(src, dst, send_sem, recv_sem, to):
        return pltpu.make_async_remote_copy(
            src_ref=src, dst_ref=dst, send_sem=send_sem, recv_sem=recv_sem, device_id=to, device_id_type=MESH
        )

    def send_column(a):
        at = dp * n_owner + me
        pltpu.make_async_copy(args[a].at[me], weights.at[a, at], w_recv.at[a, 0, 0]).start()
        for r in range(1, n_owner):
            to = ((half + r // n_half) % 2) * n_half + (low + r) % n_half
            remote(args[a].at[to], weights.at[a, at], z_send.at[a], w_recv.at[a, r, 0], (dp, to)).start()

    def send_half():
        for t in range(n_half):
            to = (low + t) % n_half
            for b in range(2):
                src = down_ref.at[b * n_half + to]
                slot = low * 2 + b
                dst, arrive = weights.at[2, dp * n_owner + slot], w_recv.at[2, slot, 0]
                if t == 0:
                    pltpu.make_async_copy(src, dst, arrive).start()
                else:
                    remote(src, dst, z_send.at[2], arrive, (dp, half * n_half + to)).start()

    def piece(a, r, part):
        if a == 2:
            return weights.at[2, part * n_owner + r]
        source = ((half + r // n_half) % 2) * n_half + (low + n_owner - r) % n_half
        return weights.at[a, part * n_owner + source]

    def spread(a, r, part, to, slot, kind):
        held = piece(a, r, part)
        remote(held, held, xy_send.at[a, kind], w_recv.at[a, r, slot], (to, me)).start()

    def arrived(a, r, part, slot):
        wait_bytes(piece(a, r, part), w_recv.at[a, r, slot])

    def relay(a, r):
        arrived(a, r, dp, 0)
        spread(a, r, dp, x_dp, 1, 0)
        spread(a, r, dp, y_dp, 2, 1)

    def corner(a, r):
        arrived(a, r, x_dp, 1)
        if r % 2 == 0:
            spread(a, r, x_dp, y_dp, 3, 2)
        arrived(a, r, y_dp, 2)
        if r % 2 == 1:
            spread(a, r, y_dp, x_dp, 3, 2)

    send_column(0)
    relay(0, 0)

    block = 16

    @pl.loop(0, tok_dev // block)
    def _(i):
        at = pl.ds(pl.multiple_of(i * block, block), block)
        values = tok_ref[at, :].astype(jnp.float32)
        meansq = jnp.mean(values * values, axis=-1, keepdims=True)
        fresh = values * lax.rsqrt(meansq + EPS) * (1.0 + scale_ref[...]) + shift_ref[...]
        normed[at, :] = fresh.astype(jnp.bfloat16)

    remote(normed, far_tok, f_send.at[0], f_recv.at[0], (dp, mirror)).start()
    logits = jnp.dot(normed[...], router_ref[...], preferred_element_type=jnp.float32)
    names = lax.broadcasted_iota(jnp.int32, logits.shape, 1)
    lanes = lax.broadcasted_iota(jnp.int32, meta.shape[1:], 1)
    facts = jnp.zeros(meta.shape[1:], jnp.float32)
    for k in range(2):
        chosen = jnp.sum(jnp.where(routes_ref[:, k : k + 1] == names, logits, 0.0), axis=-1, keepdims=True)
        facts = jnp.where(lanes == k, place_ref[:, k : k + 1].astype(jnp.float32), facts)
        facts = jnp.where(lanes == 2 + k, jax.nn.sigmoid(chosen), facts)
    meta[0] = facts
    remote(meta.at[0], meta.at[1], f_send.at[1], f_recv.at[1], (dp, mirror)).start()

    def dispatch(who):
        source = normed if who == 0 else far_tok
        from_half = half if who == 0 else other
        for t in range(n_half):
            to = (low + t) % n_half
            expert = half * n_half + to
            spots = (expert * capacity + lax.broadcasted_iota(jnp.int32, (tok_dev, capacity), 1)).astype(jnp.float32)
            first = jnp.where(meta[who, :, 0:1] == spots, 1.0, 0.0)
            second = jnp.where(meta[who, :, 1:2] == spots, 1.0, 0.0)
            hot = (first + second).astype(jnp.bfloat16)
            picked = lax.dot_general(
                hot, source[...], (((0,), (0,)), ((), ())), preferred_element_type=jnp.float32
            ).astype(jnp.bfloat16)
            if t == 0:
                rows[low, from_half] = picked
            else:
                outgoing[who, t - 1] = picked
                remote(
                    outgoing.at[who, t - 1], rows.at[low, from_half],
                    t_send.at[who], t_recv.at[who, t], (dp, expert),
                ).start()

    dispatch(0)
    send_column(1)
    send_half()

    def take_far():
        wait_bytes(far_tok, f_recv.at[0])
        wait_bytes(meta.at[1], f_recv.at[1])
        dispatch(1)
        for who in range(2):
            cells = lax.broadcasted_iota(jnp.int32, comb.shape[2:], 1).astype(jnp.float32)
            for k in range(2):
                comb[who, k] = jnp.where(meta[who, :, k : k + 1] == cells, 1.0, 0.0).astype(jnp.bfloat16)

    tile = 256

    def multiply(a):
        for r in range(n_owner):
            arrived(a, r, d_dp, 3)
        if a == 0:
            for who in range(2):
                from_half = half if who == 0 else other
                for t in range(1, n_half):
                    wait_bytes(rows.at[(low + n_half - t) % n_half, from_half], t_recv.at[who, t])

        @pl.loop(0, units // tile)
        def _(i):
            at = pl.ds(pl.multiple_of(i * tile, tile), tile)
            part = weights[a, :, :, at].reshape(width, tile)
            grid = rows[...].reshape(n_owner * capacity, width)
            result = jnp.dot(grid, part, preferred_element_type=jnp.float32)
            if a == 0:
                gate_acc[:, at] = result
            else:
                hidden[half, :, at] = (jax.nn.silu(gate_acc[:, at]) * result).astype(jnp.bfloat16)

        if a == 1:
            remote(hidden.at[half], hidden.at[half], h_sem.at[0], h_sem.at[1], (dp, mirror)).start()

    def finish(s):
        if s == 0:
            wait_bytes(hidden.at[other], h_sem.at[1])
        for b in range(2):
            r = s * 2 + b
            arrived(2, r, d_dp, 3)
            for q in range(n_dp):
                result = lax.dot_general(
                    hidden[b], weights[2, q * n_owner + r], (((1,), (1,)), ((), ())),
                    preferred_element_type=jnp.float32,
                ).astype(jnp.bfloat16)
                obuf[s, b, :, :, :, q * depth : (q + 1) * depth] = result.reshape(n_half, 2, capacity, depth)
            incoming[s, b * n_half + low] = obuf[s, b, low]
            for t in range(1, n_half):
                to = (low + t) % n_half
                remote(
                    obuf.at[s, b, to], incoming.at[s, b * n_half + low],
                    o_send.at[s], o_recv.at[s, b, t], (dp, half * n_half + to),
                ).start()

    def columns(q, part, s):
        return pl.ds(pl.multiple_of(((q * 2 + part) * n_half + s) * depth, depth), depth)

    def combine(s):
        for b in range(2):
            for t in range(1, n_half):
                sender = b * n_half + (low + n_half - t) % n_half
                wait_bytes(incoming.at[s, sender], o_recv.at[s, b, t])
        for who in (1, 0):
            block_in = incoming[s, :, half if who == 0 else other].reshape(n_owner * capacity, n_dp * depth)
            first = jnp.dot(comb[who, 0], block_in, preferred_element_type=jnp.float32)
            second = jnp.dot(comb[who, 1], block_in, preferred_element_type=jnp.float32)
            branch = meta[who, :, 2:3] * first + meta[who, :, 3:4] * second
            for q in range(n_dp):
                at = columns(q, half, s)
                value = (gmod_ref[:, at] * branch[:, q * depth : (q + 1) * depth]).astype(jnp.bfloat16)
                if who == 0:
                    out_ref[:, at] = value
                else:
                    dense[s, :, q * depth : (q + 1) * depth] = value
            if who == 1:
                remote(dense.at[s], land.at[s], d_send.at[0], d_recv.at[s], (dp, mirror)).start()

    lag, far = LAG, FAR
    pieces = 3 * n_owner
    for k in range(1, pieces + lag + far):
        if k == n_owner + FAR_TOKENS:
            take_far()
        if k < pieces:
            relay(*divmod(k, n_owner))
        if lag <= k < pieces + lag:
            corner(*divmod(k - lag, n_owner))
        if k >= lag + far:
            a, r = divmod(k - lag - far, n_owner)
            if (a, r) == (1, GATE_AT):
                multiply(0)
            if (a, r) == (1, n_owner - 1):
                multiply(1)
            if a == 2 and r % 2 == 1:
                finish(r // 2)
                if r > 1:
                    combine(r // 2 - 1)
    combine(n_half - 1)
    for s in range(n_half):
        wait_bytes(land.at[s], d_recv.at[s])
        for q in range(n_dp):
            out_ref[:, columns(q, other, s)] = land[s, :, q * depth : (q + 1) * depth]

    for a in range(3):
        count = n_owner - 1 if a < 2 else n_owner - 2
        wait_bytes(args[a].at[pl.ds(0, count)], z_send.at[a])
        for kind in range(3):
            wait_bytes(weights.at[a, pl.ds(0, n_owner)], xy_send.at[a, kind])
    wait_bytes(normed, f_send.at[0])
    wait_bytes(meta.at[0], f_send.at[1])
    for who in range(2):
        wait_bytes(outgoing.at[who], t_send.at[who])
    wait_bytes(hidden.at[half], h_sem.at[0])
    for s in range(n_half):
        wait_bytes(incoming.at[s, pl.ds(0, n_owner - 2)], o_send.at[s])
    wait_bytes(dense, d_send.at[0])


def shards(
    n_dp, n_owner, tokens, routes, router_weight, shift, scale, gate_mod, gate_weight, up_weight, down_weight
):
    tok_dev, width = tokens.shape
    experts, depth, units = gate_weight.shape
    capacity = max(2, 3 * tok_dev // experts)
    first_row = (lax.axis_index("dp") * n_owner + lax.axis_index("expert")) * tok_dev
    image = first_row // PIX if shift.shape[0] > 1 else 0
    shift_row = lax.dynamic_slice_in_dim(shift, image, 1, 0)
    scale_row = lax.dynamic_slice_in_dim(scale, image, 1, 0)
    gate_row = lax.dynamic_slice_in_dim(gate_mod, image, 1, 0)
    hot = routes[:, :, None] == jnp.arange(experts, dtype=jnp.int32)[None, None, :]
    named = jnp.sum(hot.astype(jnp.bfloat16), axis=1)
    order = jnp.arange(tok_dev)
    below = (order[:, None] > order[None, :]).astype(jnp.bfloat16)
    rank = jnp.dot(below, named, preferred_element_type=jnp.float32)
    slot = jnp.sum(jnp.where(hot, rank[:, None, :], 0.0), axis=-1).astype(jnp.int32)
    place = routes * capacity + slot
    vmem = pl.BlockSpec(memory_space=pltpu.VMEM)
    hbm = pl.BlockSpec(memory_space=pl.ANY)
    grid_rows = n_owner * capacity
    n_half = n_owner // 2
    return pl.pallas_call(
        functools.partial(kernel, n_dp, n_owner),
        out_shape=jax.ShapeDtypeStruct((tok_dev, width), jnp.bfloat16),
        in_specs=[vmem] * 7 + [hbm] * 3,
        out_specs=vmem,
        scratch_shapes=[
            pltpu.VMEM((3, n_dp * n_owner, depth, units), jnp.bfloat16),
            pltpu.VMEM((tok_dev, width), jnp.bfloat16),
            pltpu.VMEM((tok_dev, width), jnp.bfloat16),
            pltpu.VMEM((2, tok_dev, 128), jnp.float32),
            pltpu.VMEM((2, n_half - 1, capacity, width), jnp.bfloat16),
            pltpu.VMEM((n_half, 2, capacity, width), jnp.bfloat16),
            pltpu.VMEM((grid_rows, units), jnp.float32),
            pltpu.VMEM((2, grid_rows, units), jnp.bfloat16),
            pltpu.VMEM((n_half, 2, n_half, 2, capacity, n_dp * depth), jnp.bfloat16),
            pltpu.VMEM((n_half, n_owner, 2, capacity, n_dp * depth), jnp.bfloat16),
            pltpu.VMEM((2, 2, tok_dev, grid_rows), jnp.bfloat16),
            pltpu.VMEM((n_half, tok_dev, n_dp * depth), jnp.bfloat16),
            pltpu.VMEM((n_half, tok_dev, n_dp * depth), jnp.bfloat16),
            pltpu.SemaphoreType.DMA((3,)),
            pltpu.SemaphoreType.DMA((3, n_owner, 4)),
            pltpu.SemaphoreType.DMA((3, 3)),
            pltpu.SemaphoreType.DMA((2,)),
            pltpu.SemaphoreType.DMA((2,)),
            pltpu.SemaphoreType.DMA((2,)),
            pltpu.SemaphoreType.DMA((2, n_half)),
            pltpu.SemaphoreType.DMA((2,)),
            pltpu.SemaphoreType.DMA((n_half,)),
            pltpu.SemaphoreType.DMA((n_half, 2, n_half)),
            pltpu.SemaphoreType.DMA((1,)),
            pltpu.SemaphoreType.DMA((n_half,)),
        ],
        compiler_params=pltpu.CompilerParams(
            collective_id=0, has_side_effects=True, vmem_limit_bytes=64000 * 1024
        ),
    )(
        tokens, router_weight, routes, place, shift_row, scale_row, gate_row,
        gate_weight, up_weight, down_weight,
    )


def choose(mesh):
    n_dp, n_owner = mesh.shape["dp"], mesh.shape["expert"]

    def body(*args):
        tokens, weight = args[0], args[6]
        capacity = max(2, 3 * tokens.shape[0] // weight.shape[0])
        fits = n_dp == 4 and weight.shape[0] == n_owner and n_owner % 2 == 0
        fits = fits and capacity % 16 == 0 and weight.shape[1] % 128 == 0 and tokens.shape[0] % 16 == 0
        fits = fits and PIX % (n_owner * tokens.shape[0]) == 0
        if fits:
            return shards(n_dp, n_owner, *args)
        return shards_plain(*args)

    return body


def solution(mesh):
    in_specs = (
        P(("dp", "expert"), None),
        P(("dp", "expert"), None),
        P(),
        P(),
        P(),
        P(),
        P(None, ("dp", "expert"), None),
        P(None, ("dp", "expert"), None),
        P(None, ("dp", "expert"), None),
    )
    out_specs = P(("dp", "expert"), None)
    return jax.shard_map(
        choose(mesh), mesh=mesh, in_specs=in_specs, out_specs=out_specs, check_vma=False)
```

time: 338 us -> 284 us (0.84)
  Pallas kernels: 328 us -> 275 us
    pallas_call x1, Pallas kernels: 328 us -> 275 us  [shards(): pl.pallas_call(functools.partial(kernel, n_dp, n_owner), out_shape=jax.Sh...]
where the time goes in v2:
time: 284 us; the launch traced here: 283 us
  Pallas kernels  275 us (97%)
  local copies, waits for them, and re-layouts  6.57 us (2%)
    pallas_call x1, Pallas kernels, shards(): pl.pallas_call(functools.partial(kernel, n_dp, n_owner), out_shape=jax.Sh...  275 us
    unnamed x3, local copies, waits for them, and re-layouts  5.84 us

profile of v2, /device:TPU:0, one launch (start us, length us, event | category | flops | bytes accessed | tf_op | source)
XLA Modules:
  0.0 283.4 jit_solution(8129333521932988320)
XLA Ops:
  0.0 0.7 fusion.2
  0.7 0.1 fusion
  0.8 0.7 select_reduce_fusion
  1.5 0.7 convert_add_fusion
  2.2 0.7 copy.23.place_ref
  2.9 1.4 copy.22.routes_ref
  4.3 2.2 copy.21.router_ref
  6.5 274.6 %shard_map.91 = bf16[128,4096]{1,0:T(8,128)(2,1)} custom-call(bf16[128,4096]{1,0:T(8,128)(2,1)} %tok_ref.1, bf16[4096,8]{1,0:T(8,128)(2,1)} %copy.21.router_ref, s32[128,2]{1,0:T(8,128)} %copy.22.routes_ref, s32[128,2]{1,0:T(8,128)} %copy.23.place_ref, f32[1,4096]{1,0:T(1,128)} %shift_ref.1, f32[1,4096]{1,0:T(1,128)} %scale_ref.1, f32[1,4096]{1,0:T(1,128)} %gmod_ref.1, ...), custom_call_target="tpu_custom_call" | custom-call | tf_op jit(solution)/shard_map/pallas_call | solution.py:361
  281.1 2.3 copy.25

commit v3 on v2

--- a/solution.py
+++ b/solution.py
@@ -12,8 +12,10 @@
 
 EPS = 1e-06
 
-LAG, FAR = 2, 1
-FAR_TOKENS, GATE_AT = 2, 3
+LAG, FAR = 1, 1
+ISSUE = (1, 1)
+FAR_TOKENS = 12
+MULTIPLY = (13, 15)
 
 
 def send_back(output):
@@ -95,8 +97,8 @@
 def kernel(
     n_dp, n_owner, tok_ref, router_ref, routes_ref, place_ref, shift_ref, scale_ref, gmod_ref,
     gate_ref, up_ref, down_ref, out_ref,
-    weights, normed, far_tok, meta, outgoing, rows, gate_acc, hidden, obuf, incoming, comb, dense, land,
-    z_send, w_recv, xy_send, f_send, f_recv, t_send, t_recv, h_sem, o_send, o_recv, d_send, d_recv,
+    weights, downs, normed, far_tok, meta, outgoing, rows, gate_acc, hidden, obuf, incoming, comb, dense, land,
+    z_send, w_recv, xy_send, f_send, f_recv, t_send, t_recv, h_send, h_recv, o_send, o_recv, d_send, d_recv,
 ):
     dp, me = lax.axis_index("dp"), lax.axis_index("expert")
     x_dp = dp + 1 - 2 * (dp % 2)
@@ -109,7 +111,11 @@
     tok_dev, width = tok_ref.shape
     capacity = outgoing.shape[2]
     depth, units = gate_ref.shape[1], gate_ref.shape[2]
-    args = (gate_ref, up_ref, down_ref)
+    span = units
+    last = 2
+
+    def argument(a, expert):
+        return (gate_ref, up_ref)[a].at[expert]
 
     barrier = pltpu.get_barrier_semaphore()
     for r in range(1, n_owner):
@@ -125,26 +131,26 @@
 
     def send_column(a):
         at = dp * n_owner + me
-        pltpu.make_async_copy(args[a].at[me], weights.at[a, at], w_recv.at[a, 0, 0]).start()
+        pltpu.make_async_copy(argument(a, me), weights.at[a, at], w_recv.at[a, 0, 0]).start()
         for r in range(1, n_owner):
             to = ((half + r // n_half) % 2) * n_half + (low + r) % n_half
-            remote(args[a].at[to], weights.at[a, at], z_send.at[a], w_recv.at[a, r, 0], (dp, to)).start()
+            remote(argument(a, to), weights.at[a, at], z_send.at[a], w_recv.at[a, r, 0], (dp, to)).start()
 
     def send_half():
-        for t in range(n_half):
-            to = (low + t) % n_half
-            for b in range(2):
-                src = down_ref.at[b * n_half + to]
-                slot = low * 2 + b
-                dst, arrive = weights.at[2, dp * n_owner + slot], w_recv.at[2, slot, 0]
+        for b in range(2):
+            for t in range(n_half):
+                to = (low + t) % n_half
+                src = down_ref.at[((half + b) % 2) * n_half + to]
+                slot = b * n_half + low
+                dst, arrive = downs.at[dp * n_owner + slot], w_recv.at[last, slot, 0]
                 if t == 0:
                     pltpu.make_async_copy(src, dst, arrive).start()
                 else:
-                    remote(src, dst, z_send.at[2], arrive, (dp, half * n_half + to)).start()
+                    remote(src, dst, z_send.at[last], arrive, (dp, half * n_half + to)).start()
 
     def piece(a, r, part):
-        if a == 2:
-            return weights.at[2, part * n_owner + r]
+        if a == last:
+            return downs.at[part * n_owner + r]
         source = ((half + r // n_half) % 2) * n_half + (low + n_owner - r) % n_half
         return weights.at[a, part * n_owner + source]
 
@@ -216,8 +222,6 @@
                 ).start()
 
     dispatch(0)
-    send_column(1)
-    send_half()
 
     def take_far():
         wait_bytes(far_tok, f_recv.at[0])
@@ -239,39 +243,43 @@
                 for t in range(1, n_half):
                     wait_bytes(rows.at[(low + n_half - t) % n_half, from_half], t_recv.at[who, t])
 
-        @pl.loop(0, units // tile)
+        @pl.loop(0, span // tile)
         def _(i):
             at = pl.ds(pl.multiple_of(i * tile, tile), tile)
             part = weights[a, :, :, at].reshape(width, tile)
             grid = rows[...].reshape(n_owner * capacity, width)
             result = jnp.dot(grid, part, preferred_element_type=jnp.float32)
-            if a == 0:
+            if a % 2 == 0:
                 gate_acc[:, at] = result
             else:
-                hidden[half, :, at] = (jax.nn.silu(gate_acc[:, at]) * result).astype(jnp.bfloat16)
-
-        if a == 1:
-            remote(hidden.at[half], hidden.at[half], h_sem.at[0], h_sem.at[1], (dp, mirror)).start()
-
-    def finish(s):
-        if s == 0:
-            wait_bytes(hidden.at[other], h_sem.at[1])
-        for b in range(2):
-            r = s * 2 + b
-            arrived(2, r, d_dp, 3)
-            for q in range(n_dp):
-                result = lax.dot_general(
-                    hidden[b], weights[2, q * n_owner + r], (((1,), (1,)), ((), ())),
-                    preferred_element_type=jnp.float32,
-                ).astype(jnp.bfloat16)
-                obuf[s, b, :, :, :, q * depth : (q + 1) * depth] = result.reshape(n_half, 2, capacity, depth)
-            incoming[s, b * n_half + low] = obuf[s, b, low]
-            for t in range(1, n_half):
-                to = (low + t) % n_half
-                remote(
-                    obuf.at[s, b, to], incoming.at[s, b * n_half + low],
-                    o_send.at[s], o_recv.at[s, b, t], (dp, half * n_half + to),
-                ).start()
+                hidden[0, a // 2, :, at] = (jax.nn.silu(gate_acc[:, at]) * result).astype(jnp.bfloat16)
+
+        if a % 2 == 1:
+            remote(hidden.at[0, a // 2], hidden.at[1, a // 2], h_send.at[a // 2], h_recv.at[a // 2], (dp, mirror)).start()
+
+    def finish(r):
+        b, s = divmod(r, n_half)
+        if r == n_half:
+            for side in range(1):
+                wait_bytes(hidden.at[1, side], h_recv.at[side])
+        arrived(last, r, d_dp, 3)
+        expert = ((half + b) % 2) * n_half + low
+        for q in range(n_dp):
+            total = jnp.zeros((n_owner * capacity, depth), jnp.float32)
+            for side in range(1):
+                total += lax.dot_general(
+                    hidden[b, side], downs[q * n_owner + r, :, side * span : (side + 1) * span],
+                    (((1,), (1,)), ((), ())), preferred_element_type=jnp.float32,
+                )
+            result = total.astype(jnp.bfloat16).reshape(n_half, 2, capacity, depth)
+            obuf[r, :, :, :, q * depth : (q + 1) * depth] = result
+        incoming[s, expert] = obuf[r, low]
+        for t in range(1, n_half):
+            to = (low + t) % n_half
+            remote(
+                obuf.at[r, to], incoming.at[s, expert],
+                o_send.at[r], o_recv.at[s, b, t], (dp, half * n_half + to),
+            ).start()
 
     def columns(q, part, s):
         return pl.ds(pl.multiple_of(((q * 2 + part) * n_half + s) * depth, depth), depth)
@@ -279,7 +287,7 @@
     def combine(s):
         for b in range(2):
             for t in range(1, n_half):
-                sender = b * n_half + (low + n_half - t) % n_half
+                sender = ((half + b) % 2) * n_half + (low + n_half - t) % n_half
                 wait_bytes(incoming.at[s, sender], o_recv.at[s, b, t])
         for who in (1, 0):
             block_in = incoming[s, :, half if who == 0 else other].reshape(n_owner * capacity, n_dp * depth)
@@ -297,42 +305,45 @@
                 remote(dense.at[s], land.at[s], d_send.at[0], d_recv.at[s], (dp, mirror)).start()
 
     lag, far = LAG, FAR
-    pieces = 3 * n_owner
-    for k in range(1, pieces + lag + far):
-        if k == n_owner + FAR_TOKENS:
+    steps = [(a, r) for a in range(last + 1) for r in range(n_owner)]
+    for k in range(1, len(steps) + lag + far):
+        for a in range(1, last + 1):
+            if k == ISSUE[a - 1]:
+                send_half() if a == last else send_column(a)
+        if k == FAR_TOKENS:
             take_far()
-        if k < pieces:
-            relay(*divmod(k, n_owner))
-        if lag <= k < pieces + lag:
-            corner(*divmod(k - lag, n_owner))
+        if k < len(steps):
+            relay(*steps[k])
+        if lag <= k < len(steps) + lag:
+            corner(*steps[k - lag])
         if k >= lag + far:
-            a, r = divmod(k - lag - far, n_owner)
-            if (a, r) == (1, GATE_AT):
-                multiply(0)
-            if (a, r) == (1, n_owner - 1):
-                multiply(1)
-            if a == 2 and r % 2 == 1:
-                finish(r // 2)
-                if r > 1:
-                    combine(r // 2 - 1)
+            a, r = steps[k - lag - far]
+            for half_step in range(last):
+                if (a * n_owner + r) == MULTIPLY[half_step]:
+                    multiply(half_step)
+            if a == last:
+                finish(r)
+                if r > n_half:
+                    combine(r - n_half - 1)
     combine(n_half - 1)
     for s in range(n_half):
         wait_bytes(land.at[s], d_recv.at[s])
         for q in range(n_dp):
             out_ref[:, columns(q, other, s)] = land[s, :, q * depth : (q + 1) * depth]
 
-    for a in range(3):
-        count = n_owner - 1 if a < 2 else n_owner - 2
-        wait_bytes(args[a].at[pl.ds(0, count)], z_send.at[a])
+    for a in range(last + 1):
+        held = downs if a == last else weights.at[a]
+        wait_bytes(held.at[pl.ds(0, n_owner - 2 if a == last else n_owner - 1)], z_send.at[a])
         for kind in range(3):
-            wait_bytes(weights.at[a, pl.ds(0, n_owner)], xy_send.at[a, kind])
+            wait_bytes(held.at[pl.ds(0, n_owner)], xy_send.at[a, kind])
     wait_bytes(normed, f_send.at[0])
     wait_bytes(meta.at[0], f_send.at[1])
     for who in range(2):
         wait_bytes(outgoing.at[who], t_send.at[who])
-    wait_bytes(hidden.at[half], h_sem.at[0])
-    for s in range(n_half):
-        wait_bytes(incoming.at[s, pl.ds(0, n_owner - 2)], o_send.at[s])
+    for side in range(1):
+        wait_bytes(hidden.at[0, side], h_send.at[side])
+    for r in range(n_owner):
+        wait_bytes(obuf.at[r, pl.ds(0, n_half - 1)], o_send.at[r])
     wait_bytes(dense, d_send.at[0])
 
 
@@ -364,15 +375,16 @@
         in_specs=[vmem] * 7 + [hbm] * 3,
         out_specs=vmem,
         scratch_shapes=[
-            pltpu.VMEM((3, n_dp * n_owner, depth, units), jnp.bfloat16),
+            pltpu.VMEM((2, n_dp * n_owner, depth, units), jnp.bfloat16),
+            pltpu.VMEM((n_dp * n_owner, depth, units), jnp.bfloat16),
             pltpu.VMEM((tok_dev, width), jnp.bfloat16),
             pltpu.VMEM((tok_dev, width), jnp.bfloat16),
             pltpu.VMEM((2, tok_dev, 128), jnp.float32),
             pltpu.VMEM((2, n_half - 1, capacity, width), jnp.bfloat16),
             pltpu.VMEM((n_half, 2, capacity, width), jnp.bfloat16),
             pltpu.VMEM((grid_rows, units), jnp.float32),
-            pltpu.VMEM((2, grid_rows, units), jnp.bfloat16),
-            pltpu.VMEM((n_half, 2, n_half, 2, capacity, n_dp * depth), jnp.bfloat16),
+            pltpu.VMEM((2, 1, grid_rows, units), jnp.bfloat16),
+            pltpu.VMEM((n_owner, n_half, 2, capacity, n_dp * depth), jnp.bfloat16),
             pltpu.VMEM((n_half, n_owner, 2, capacity, n_dp * depth), jnp.bfloat16),
             pltpu.VMEM((2, 2, tok_dev, grid_rows), jnp.bfloat16),
             pltpu.VMEM((n_half, tok_dev, n_dp * depth), jnp.bfloat16),
@@ -384,8 +396,9 @@
             pltpu.SemaphoreType.DMA((2,)),
             pltpu.SemaphoreType.DMA((2,)),
             pltpu.SemaphoreType.DMA((2, n_half)),
-            pltpu.SemaphoreType.DMA((2,)),
-            pltpu.SemaphoreType.DMA((n_half,)),
+            pltpu.SemaphoreType.DMA((1,)),
+            pltpu.SemaphoreType.DMA((1,)),
+            pltpu.SemaphoreType.DMA((n_owner,)),
             pltpu.SemaphoreType.DMA((n_half, 2, n_half)),
             pltpu.SemaphoreType.DMA((1,)),
             pltpu.SemaphoreType.DMA((n_half,)),
@@ -407,7 +420,7 @@
         capacity = max(2, 3 * tokens.shape[0] // weight.shape[0])
         fits = n_dp == 4 and weight.shape[0] == n_owner and n_owner % 2 == 0
         fits = fits and capacity % 16 == 0 and weight.shape[1] % 128 == 0 and tokens.shape[0] % 16 == 0
-        fits = fits and PIX % (n_owner * tokens.shape[0]) == 0
+        fits = fits and weight.shape[2] % 512 == 0 and PIX % (n_owner * tokens.shape[0]) == 0
         if fits:
             return shards(n_dp, n_owner, *args)
         return shards_plain(*args)

time: 284 us -> 269 us (0.947)
  Pallas kernels: 275 us -> 260 us
    pallas_call x1, Pallas kernels: 275 us -> 260 us  [shards(): pl.pallas_call(functools.partial(kernel, n_dp, n_owner), out_shape=jax.Sh...]
where the time goes in v3:
time: 269 us
  Pallas kernels  260 us (97%)
  local copies, waits for them, and re-layouts  6.57 us (2%)
    pallas_call x1, Pallas kernels, shards(): pl.pallas_call(functools.partial(kernel, n_dp, n_owner), out_shape=jax.Sh...  260 us
    unnamed x3, local copies, waits for them, and re-layouts  5.84 us

profile of v3, /device:TPU:0, one launch (start us, length us, event | category | flops | bytes accessed | tf_op | source)
XLA Modules:
  0.0 269.0 jit_solution(14247966916743081509)
XLA Ops:
  0.0 0.7 fusion.2
  0.7 0.1 fusion
  0.8 0.7 select_reduce_fusion
  1.5 0.7 convert_add_fusion
  2.2 0.7 copy.23.place_ref
  2.9 1.4 copy.22.routes_ref
  4.3 2.2 copy.21.router_ref
  6.5 260.2 %shard_map.91 = bf16[128,4096]{1,0:T(8,128)(2,1)} custom-call(bf16[128,4096]{1,0:T(8,128)(2,1)} %tok_ref.1, bf16[4096,8]{1,0:T(8,128)(2,1)} %copy.21.router_ref, s32[128,2]{1,0:T(8,128)} %copy.22.routes_ref, s32[128,2]{1,0:T(8,128)} %copy.23.place_ref, f32[1,4096]{1,0:T(1,128)} %shift_ref.1, f32[1,4096]{1,0:T(1,128)} %scale_ref.1, f32[1,4096]{1,0:T(1,128)} %gmod_ref.1, ...), custom_call_target="tpu_custom_call" | custom-call | tf_op jit(solution)/shard_map/pallas_call | solution.py:372
  266.8 2.3 copy.25
